TPU v7x, 32 devices: a whole 2x2x4 slice. The times are simulated.
32 devices in a mesh: seq: 32 (over z, y, x, core).
Axes of the slice: x: 2, y: 2, z: 4, core: 2. Of those that a mesh axis runs over, the one named last changes fastest.
Arguments:
- queries: bfloat16 [2, 4, 128, 576], replicated, may hold values from -40 to 40
- latent_cache: bfloat16 [2, 131072, 576], P(None, 'seq'), may hold values from -6 to 6
- lengths: int32 [2], replicated, may hold values from 16384 to 131072
- offsets: int32 [2, 4], replicated, may hold values from 0 to 3
Outputs:
- attended: bfloat16 [2, 4, 128, 512], replicated
All inputs are finite; a program needn't handle non-finite values.
Results may differ from a plain program's by a relative error of at most 0.001.
The roundings to bfloat16 on the way count: a program that leaves them out, or rounds other values in their place, can miss the bound.
Values may be sent and summed in bfloat16 or wider, within the bound.
A program may use at most 128 MiB of HBM per device.

v0:
```python
import jax
import jax.numpy as jnp
from jax import lax
from jax.sharding import PartitionSpec as P

LATENT = 512


softmax_scale = 192.0 ** (-0.5)


def block_partial(rows, cache, limit, start):
    score = jnp.dot(rows, cache.T, preferred_element_type=jnp.float32) * softmax_scale
    places = start + jnp.arange(cache.shape[0], dtype=jnp.int32)
    visible = places[None, :] < limit[:, None]
    score = jnp.where(visible, score, -1e30)
    peak = jnp.max(score, axis=1)
    weight = jnp.where(visible, jnp.exp(score - peak[:, None]), 0.0)
    total = jnp.sum(weight, axis=1)
    partial_value = jnp.dot(
        weight.astype(jnp.bfloat16), cache[:, :LATENT], preferred_element_type=jnp.float32
    )
    return (peak, total, partial_value)


def on_device(queries, latent_cache, lengths, offsets):
    requests, qtokens, heads, width = queries.shape
    cache_dev = latent_cache.shape[1]
    start = lax.axis_index("seq") * cache_dev
    rows = queries.reshape(requests, qtokens * heads, width)
    limits = jnp.repeat(lengths[:, None] - qtokens + 1 + offsets, heads, axis=1)

    def compute(operands):
        return block_partial(operands[0], operands[1], operands[2], start)

    peak, total, partial_value = jax.vmap(compute)((rows, latent_cache, limits))
    flat_count = requests * qtokens * heads
    peak = peak.reshape(flat_count)
    total = total.reshape(flat_count)
    partial_value = partial_value.reshape(flat_count, LATENT)
    top = lax.pmax(peak, "seq")
    factor = jnp.exp(peak - top)
    upper, lower = lax.psum((partial_value * factor[:, None], total * factor), "seq")
    finished = (upper / lower[:, None]).astype(jnp.bfloat16)
    return finished.reshape(requests, qtokens, heads, LATENT)


def solution(mesh):
    placed = (P(), P(None, "seq", None), P(), P())
    return jax.shard_map(on_device, mesh=mesh, in_specs=placed, out_specs=P(), check_vma=False)
```

profile of v0, /device:TPU:0, one launch (start us, length us, event | category | flops | bytes accessed | tf_op | source)
XLA Modules:
  0.0 230.8 jit_solution(12443446857125961201)
XLA Ops:
  6.5 0.0 copy-start
  6.5 0.0 all-reduce.2.cloned.1.call-start
  6.5 0.8 broadcast_add_fusion.1
  7.3 0.7 broadcast_add_fusion
  8.0 0.1 broadcast_bitcast_fusion
  8.1 0.0 copy-done
  8.1 15.5 %fusion = (f32[2,512]{1,0:T(2,128)S(1)}, f32[2,512,4096]{2,1,0:T(8,128)}) fusion(s32[2,512]{1,0:T(2,128)S(1)} %bitcast.24, s32[4096]{0:T(1024)S(1)} %iota_add_fusion, bf16[2,4096,576]{1,2,0:T(8,128)(2,1)} %param.5, bf16[2,4,128,576]{2,3,1,0:T(8,128)(2,1)S(1)} %copy-done), kind=kOutput, calls=%fused_computation.2 | convolution fusion | flops 4848614400 | bytes 27418624 | tf_op jit(solution)/shard_map/vmap()/dot_general | solution.py:13
  23.6 10.6 %fusion.3 = f32[2,512,512]{2,1,0:T(8,128)S(1)} fusion(bf16[2,4096,576]{1,2,0:T(8,128)(2,1)} %param.5, f32[2,512,4096]{2,1,0:T(8,128)} %get-tuple-element.8, f32[2,512]{1,0:T(2,128)S(1)} %get-tuple-element.7, s32[2,512]{1,0:T(2,128)S(1)} %bitcast.25, s32[4096]{0:T(1024)S(1)} %iota_add_fusion), kind=kOutput, calls=%fused_computation.5 | convolution fusion | flops 4320133120 | bytes 27287552 | tf_op jit(solution)/shard_map/vmap()/dot_general | solution.py:20
  34.2 8.4 %fusion.1 = f32[2,512]{1,0:T(2,128)S(1)} fusion(f32[2,512,4096]{2,1,0:T(8,128)} %get-tuple-element.8, f32[2,512]{1,0:T(2,128)S(1)} %get-tuple-element.7, s32[2,512]{1,0:T(2,128)S(1)} %bitcast.26, s32[4096]{0:T(1024)S(1)} %iota_add_fusion), kind=kLoop, calls=%fused_computation.3 | loop fusion | flops 25164800 | bytes 16805888 | tf_op jit(solution)/shard_map/vmap()/reduce_sum | solution.py:19
  42.7 42.0 %pmax.7 = f32[1024]{0:T(1024)S(1)} all-reduce(f32[1024]{0:T(1024)S(1)} %bitcast.22), channel_id=1, replica_groups=mesh['seq'=32] {'seq'}, use_global_device_ids=true, to_apply=%region_1.2 | all-reduce | flops 1024 | bytes 8192 | tf_op jit(solution)/shard_map/pmax | solution.py:41
  84.7 1.5 bitcast_multiply_fusion
  86.2 0.0 all-reduce.2.cloned.1.call-update
  86.2 40.4 %psum.15 = f32[1024]{0:T(1024)S(1)} all-reduce(f32[1024]{0:T(1024)S(1)} %get-tuple-element.5), channel_id=1, replica_groups=mesh['seq'=32] {'seq'}, use_global_device_ids=true, to_apply=%region_4.5 | all-reduce | flops 1024 | bytes 8192 | tf_op jit(solution)/shard_map/psum | solution.py:43
  126.6 94.5 %all-reduce.2.cloned.1.call-done = f32[1024,512]{1,0:T(8,128)} async-done(((f32[1024,512]{1,0:T(8,128)}), f32[1024,512]{1,0:T(8,128)}) %all-reduce.2.cloned.1.call-update) | async-done | bytes 2097168 | tf_op jit(solution)/shard_map/psum | solution.py:43
  221.1 2.8 %divide_convert_fusion = bf16[1024,512]{1,0:T(8,128)(2,1)} fusion(f32[1024,512]{1,0:T(8,128)} %all-reduce.2.cloned.1.call-done, f32[1024]{0:T(1024)S(1)} %psum.15), kind=kLoop, calls=%fused_computation.13 | loop fusion | flops 1048576 | bytes 3149824 | tf_op jit(solution)/shard_map/convert_element_type | solution.py:44
  (5 shorter events, 0.0 us)
Async XLA Ops:
  6.5 1.6 copy-start
  6.5 214.6 %all-reduce.2.cloned.1.call-start = ((), (), s32[]{:S(2)}) async-start(), calls=%async_computation | async-start | bytes 4194304 | tf_op jit(solution)/shard_map/psum | solution.py:43
Sparse Core Ops, SparseCore 0:
  86.3 134.7 all-reduce.1
where the time goes:
time: 231 us
  waiting for transfers between devices  94.5 us (41%)
  blocking collectives  82.4 us (36%)
  matrix products  26.1 us (11%)
  other arithmetic  14.2 us (6%)
  between operations  13.4 us (6%)
    psum x1, waiting for transfers between devices, on_device(): lax.psum((partial_value * factor[:, None], total * factor), 'seq')  94.5 us
    pmax x1, blocking collectives, on_device(): top = lax.pmax(peak, 'seq')  42 us
    psum x1, blocking collectives, on_device(): lax.psum((partial_value * factor[:, None], total * factor), 'seq')  40.4 us
    dot_general x1, matrix products, block_partial(): jnp.dot(rows, cache.T, preferred_element_type=jnp.float32) * softmax_scale  15.5 us
    dot_general x1, matrix products, block_partial(): jnp.dot(weight.astype(jnp.bfloat16), cache[:, :LATENT], preferred_element...  10.6 us
    reduce_sum x1, other arithmetic, block_partial(): total = jnp.sum(weight, axis=1)  8.4 us
  transfers between devices with their start and end apart: 1, of which 1 were waited for; matrix products, arithmetic and copies ran while one was open for 0% of the time, Pallas kernels for 0%

commit v1 on v0

v1 whole, which is shorter than its diff:
```python
import functools

import jax
import jax.numpy as jnp
from jax import lax
from jax.experimental import pallas as pl
from jax.experimental.pallas import tpu as pltpu
from jax.sharding import PartitionSpec as P

LATENT = 512
LANES = 128
LOG2E = 1.4426950408889634
SCALE2 = (192.0 ** (-0.5)) * LOG2E
MESH = pl.DeviceIdType.MESH


def plan(n):
    chips, radices = n // 2, []
    while chips > 1:
        radix = 4 if chips % 4 == 0 else 2
        radices.append(radix)
        chips //= radix
    return radices


def split_meta(block, half):
    return block[:, :half], block[:, half:half + 1], block[:, half + 64:half + 65]


def with_meta(ref_index, ref, value, peak, total, half):
    rows = value.shape[0]
    lane = lax.broadcasted_iota(jnp.int32, (rows, LANES), 1)
    ref[(*ref_index, slice(None), pl.ds(0, half))] = value
    ref[(*ref_index, slice(None), pl.ds(half, LANES))] = jnp.where(lane < 64, peak, total)


def combine(blocks, half):
    parts = [split_meta(block, half) for block in blocks]
    top = functools.reduce(jnp.maximum, [p[1] for p in parts])
    factors = [jnp.exp2(p[1] - top) for p in parts]
    value = sum(p[0] * f for p, f in zip(parts, factors))
    total = sum(p[2] * f for p, f in zip(parts, factors))
    return value, top, total


def kernel(n, qtok, heads, chunk, lengths, offsets, q_ref, cache_hbm, out_ref,
           kv, score, w0, core_in, works, stage_in, gathered, load_sem, send_sem, recv_sem):
    rows_all = q_ref.shape[0]
    cache_dev = kv.shape[1]
    half = LATENT // 2
    chunks = rows_all // chunk
    per_request = qtok * heads // chunk
    tokens = chunk // heads
    radices = plan(n)
    stages = len(radices)
    strides, blocks, pieces = [], [], n // 2
    stride, left = 1, pieces
    for radix in radices:
        strides.append(stride)
        stride *= radix
        left //= radix
        blocks.append(left)
    piece_rows = chunk // pieces

    me = lax.axis_index("seq")
    core = lax.rem(me, 2)
    chip = me // 2
    digits = [lax.rem(chip // s, r) for s, r in zip(strides, radices)]
    partner = me + 1 - 2 * core

    def peer(stage, d):
        other = lax.rem(digits[stage] + d, radices[stage])
        return other, me + (other - digits[stage]) * strides[stage] * 2

    barrier = pltpu.get_barrier_semaphore()
    peers = [partner]
    for stage in range(stages):
        peers += [peer(stage, d)[1] for d in range(1, radices[stage])]
    for device in peers:
        pl.semaphore_signal(barrier, inc=1, device_id=(device,), device_id_type=MESH)

    def load(b):
        return pltpu.make_async_copy(cache_hbm.at[b], kv.at[b], load_sem.at[b])

    load(0).start()
    pl.semaphore_wait(barrier, len(peers))

    start = me * cache_dev
    span = 512
    value_span = 1024

    def remote(src, dst, j, slot, device):
        return pltpu.make_async_remote_copy(
            src_ref=src, dst_ref=dst, send_sem=send_sem.at[j, slot],
            recv_sem=recv_sem.at[j, slot], device_id=(device,), device_id_type=MESH)

    def core_copy(j):
        return remote(w0.at[j, 1 - core], core_in.at[j], j, 0, partner)

    def stage_copy(j, stage, d):
        other, device = peer(stage, d)
        rows = chunk
        for r in radices[:stage + 1]:
            rows //= r
        src = works[stage].at[j, pl.ds(other * rows, rows)]
        return remote(src, stage_in[stage].at[j, d - 1], j, 1 + 3 * stage + d - 1, device)

    def first_piece(stage):
        return sum(digits[i] * blocks[i] for i in range(stage + 1))

    def gather_copy(j, stage, d):
        _, device = peer(stage, d)
        ref = gathered.at[j, core, pl.ds(first_piece(stage), blocks[stage])]
        return remote(ref, ref, j, 1 + 3 * stages + 3 * stage + d - 1, device)

    def gather_arrival(j, stage, d):
        _, device = peer(stage, d)
        origin = lax.rem(digits[stage] + radices[stage] - d, radices[stage])
        first = origin * blocks[stage]
        if stage:
            first = first + first_piece(stage - 1)
        ref = gathered.at[j, core, pl.ds(first, blocks[stage])]
        return remote(ref, ref, j, 1 + 3 * stages + 3 * stage + d - 1, device)

    def core_gather(j, which):
        ref = gathered.at[j, which]
        return remote(ref, ref, j, 1 + 6 * stages, partner)

    def compute(c):
        b = c // per_request
        first_token = lax.rem(c, per_request) * tokens
        limits = [lengths[b] - (qtok - 1) + offsets[b, first_token + t] - start for t in range(tokens)]
        q = q_ref[pl.ds(pl.multiple_of(c * chunk, chunk), chunk), :]
        peak = jnp.full((chunk, LANES), -1e30, jnp.float32)
        for j in range(cache_dev // span):
            s = lax.dot_general(q, kv[b, j * span:(j + 1) * span, :], (((1,), (1,)), ((), ())),
                                preferred_element_type=jnp.float32)
            places = lax.broadcasted_iota(jnp.int32, (heads, span), 1) + j * span
            s = jnp.concatenate(
                [jnp.where(places < limits[t], s[t * heads:(t + 1) * heads] * SCALE2, -1e30)
                 for t in range(tokens)], axis=0)
            score[:, j * span:(j + 1) * span] = s
            for i in range(span // LANES):
                peak = jnp.maximum(peak, s[:, i * LANES:(i + 1) * LANES])
        peak = jnp.max(peak, axis=1, keepdims=True)
        base = jnp.maximum(peak, -1e29)
        total = jnp.zeros((chunk, LANES), jnp.float32)
        value = jnp.zeros((chunk, LATENT), jnp.float32)
        for j in range(cache_dev // value_span):
            w = jnp.exp2(score[:, j * value_span:(j + 1) * value_span] - base)
            for i in range(value_span // LANES):
                total = total + w[:, i * LANES:(i + 1) * LANES]
            value = value + jnp.dot(w.astype(jnp.bfloat16),
                                    kv[b, j * value_span:(j + 1) * value_span, :LATENT],
                                    preferred_element_type=jnp.float32)
        total = jnp.sum(total, axis=1, keepdims=True)
        for h in range(2):
            with_meta((c, h), w0, value[:, h * half:(h + 1) * half], peak, total, half)
        core_copy(c).start()

    def receive_core(j):
        core_copy(j).wait_recv()
        value, top, total = combine([w0[j, core], core_in[j]], half)
        with_meta((j,), works[0], value, top, total, half)
        for d in range(1, radices[0]):
            stage_copy(j, 0, d).start()

    def receive_stage(j, stage):
        for d in range(1, radices[stage]):
            stage_copy(j, stage, d).wait_recv()
        rows = stage_in[stage].shape[2]
        mine = works[stage][j, pl.ds(pl.multiple_of(digits[stage] * rows, rows), rows), :]
        value, top, total = combine(
            [mine] + [stage_in[stage][j, d - 1] for d in range(1, radices[stage])], half)
        if stage + 1 < stages:
            with_meta((j,), works[stage + 1], value, top, total, half)
            for d in range(1, radices[stage + 1]):
                stage_copy(j, stage + 1, d).start()
        else:
            gathered[j, core, first_piece(stage)] = (value / total).astype(jnp.bfloat16)
            for d in range(1, radices[stage]):
                gather_copy(j, stage, d).start()

    def receive_gather(j, stage):
        for d in range(1, radices[stage]):
            gather_arrival(j, stage, d).wait_recv()
        if stage:
            for d in range(1, radices[stage - 1]):
                gather_copy(j, stage - 1, d).start()
        else:
            core_gather(j, core).start()

    def finish(j):
        core_gather(j, 1 - core).wait_recv()
        for h in range(2):
            out_ref[pl.ds(pl.multiple_of(j * chunk, chunk), chunk), h * half:(h + 1) * half] = (
                gathered[j, h].reshape(chunk, half))
        core_copy(j).wait_send()
        for stage in range(stages):
            for d in range(1, radices[stage]):
                stage_copy(j, stage, d).wait_send()
                gather_copy(j, stage, d).wait_send()
        core_gather(j, core).wait_send()

    steps = [receive_core]
    steps += [functools.partial(receive_stage, stage=s) for s in range(stages)]
    steps += [functools.partial(receive_gather, stage=s) for s in reversed(range(stages))]
    steps += [finish]

    def iteration(i, carry):
        @pl.when(i < chunks)
        def _():
            @pl.when(lax.rem(i, per_request) == 0)
            def _():
                b = i // per_request
                load(b).wait()

                @pl.when(b + 1 < kv.shape[0])
                def _():
                    load(b + 1).start()

            compute(i)

        for lag in range(len(steps), 0, -1):
            j = i - lag

            @pl.when(jnp.logical_and(j >= 0, j < chunks))
            def _():
                steps[lag - 1](j)

        return carry

    lax.fori_loop(0, chunks + len(steps), iteration, 0)


def on_device(n, queries, latent_cache, lengths, offsets):
    requests, qtok, heads, width = queries.shape
    cache_dev = latent_cache.shape[1]
    rows = requests * qtok * heads
    radices = plan(n)
    stages = len(radices)
    chunk = max(2 * heads, n // 2 * 8)
    chunks = rows // chunk
    half = LATENT // 2
    wide = half + LANES
    works, stage_in, left = [], [], chunk
    for radix in radices:
        works.append(pltpu.VMEM((chunks, left, wide), jnp.float32))
        left //= radix
        stage_in.append(pltpu.VMEM((chunks, radix - 1, left, wide), jnp.float32))
    slots = 2 + 6 * stages
    out = pl.pallas_call(
        functools.partial(kernel, n, qtok, heads, chunk),
        out_shape=jax.ShapeDtypeStruct((rows, LATENT), jnp.bfloat16),
        in_specs=[
            pl.BlockSpec(memory_space=pltpu.SMEM),
            pl.BlockSpec(memory_space=pltpu.SMEM),
            pl.BlockSpec(memory_space=pltpu.VMEM),
            pl.BlockSpec(memory_space=pl.ANY),
        ],
        out_specs=pl.BlockSpec(memory_space=pltpu.VMEM),
        scratch_shapes=[
            pltpu.VMEM((requests, cache_dev, width), jnp.bfloat16),
            pltpu.VMEM((chunk, cache_dev), jnp.float32),
            pltpu.VMEM((chunks, 2, chunk, wide), jnp.float32),
            pltpu.VMEM((chunks, chunk, wide), jnp.float32),
            works,
            stage_in,
            pltpu.VMEM((chunks, 2, n // 2, chunk // (n // 2), half), jnp.bfloat16),
            pltpu.SemaphoreType.DMA((requests,)),
            pltpu.SemaphoreType.DMA((chunks, slots)),
            pltpu.SemaphoreType.DMA((chunks, slots)),
        ],
        compiler_params=pltpu.CompilerParams(
            collective_id=0, has_side_effects=True, vmem_limit_bytes=60 * 1024 * 1024),
        name="latent_attention",
    )(lengths, offsets, queries.reshape(rows, width), latent_cache)
    return out.reshape(requests, qtok, heads, LATENT)


def solution(mesh):
    placed = (P(), P(None, "seq", None), P(), P())
    body = functools.partial(on_device, mesh.shape["seq"])
    return jax.shard_map(body, mesh=mesh, in_specs=placed, out_specs=P(), check_vma=False)
```

time: 231 us -> 73.3 us (0.32)
  waiting for transfers between devices: 94.5 us -> 0 us
  blocking collectives: 82.4 us -> 0 us
  Pallas kernels: 0 us -> 54.5 us
  matrix products: 26.1 us -> 0 us
  local copies, waits for them, and re-layouts: 0.09 us -> 18.3 us
  other arithmetic: 14.2 us -> 0 us
  between operations: 13.4 us -> 0.01 us
    psum x1 -> x0, waiting for transfers between devices: 94.5 us -> none  [on_device(): lax.psum((partial_value * factor[:, None], total * factor), 'seq')]
    pallas_call x0 -> x1, Pallas kernels: none -> 54.5 us  [on_device(): pl.pallas_call(functools.partial(kernel, n, qtok, heads, chunk), out_shap...]
    pmax x1 -> x0, blocking collectives: 42 us -> none  [on_device(): top = lax.pmax(peak, 'seq')]
    psum x1 -> x0, blocking collectives: 40.4 us -> none  [on_device(): lax.psum((partial_value * factor[:, None], total * factor), 'seq')]
    dot_general x2 -> x0, matrix products: 26.1 us -> none  [the longest x1 15.5 us: block_partial(): jnp.dot(rows, cache.T, preferred_element_type=jnp.float32) * softmax_scale]
    unnamed x6 -> x3, local copies, waits for them, and re-layouts: 0.09 us -> 18.3 us
    reduce_sum x1 -> x0, other arithmetic: 8.4 us -> none  [block_partial(): total = jnp.sum(weight, axis=1)]
    convert_element_type x1 -> x0, other arithmetic: 2.78 us -> none  [on_device(): finished = (upper / lower[:, None]).astype(jnp.bfloat16)]
  transfers between devices with their start and end apart: 1 -> 0, of which waited for: 1 -> 0; matrix products, arithmetic and copies ran while one was open for 0% -> 0% of each run, Pallas kernels for 0% -> 0%
where the time goes in v1:
time: 73.3 us; the launch traced here: 72.8 us
  Pallas kernels  54.5 us (74%)
  local copies, waits for them, and re-layouts  18.3 us (25%)
    pallas_call x1, Pallas kernels, on_device(): pl.pallas_call(functools.partial(kernel, n, qtok, heads, chunk), out_shap...  54.5 us
    unnamed x3, local copies, waits for them, and re-layouts  18.3 us

profile of v1, /device:TPU:0, one launch (start us, length us, event | category | flops | bytes accessed | tf_op | source)
XLA Modules:
  0.0 72.8 jit_solution(15754706728012426615)
XLA Ops:
  0.0 2.4 %copy.5 = bf16[2,4,128,576]{3,2,1,0:T(8,128)(2,1)} copy(bf16[2,4,128,576]{2,3,1,0:T(8,128)(2,1)} %param.4) | data formatting | bytes 2359296 | tf_op args[0]
  2.4 13.6 %copy.6.cache_hbm = bf16[2,4096,576]{2,1,0:T(8,128)(2,1)} copy(bf16[2,4096,576]{1,2,0:T(8,128)(2,1)} %param.5) | data formatting | bytes 18874368 | tf_op args[1]
  16.0 54.5 %latent_attention.1 = bf16[1024,512]{1,0:T(8,128)(2,1)} custom-call(s32[2]{0:T(128)} %lengths.1, s32[2,4]{1,0:T(2,128)} %offsets.1, bf16[1024,576]{1,0:T(8,128)(2,1)} %bitcast.2, bf16[2,4096,576]{2,1,0:T(8,128)(2,1)} %copy.6.cache_hbm), custom_call_target="tpu_custom_call" | custom-call | tf_op jit(solution)/shard_map/latent_attention/pallas_call | solution.py:252
  70.6 2.3 %copy.8 = bf16[2,4,128,512]{3,2,1,0:T(8,128)(2,1)} copy(bf16[2,4,128,512]{3,2,1,0:T(8,128)(2,1)} %bitcast.3) | data formatting | bytes 2097152

commit v2 on v1

--- a/solution.py
+++ b/solution.py
@@ -45,8 +45,8 @@
 
 def kernel(n, qtok, heads, chunk, lengths, offsets, q_ref, cache_hbm, out_ref,
            kv, score, w0, core_in, works, stage_in, gathered, load_sem, send_sem, recv_sem):
-    rows_all = q_ref.shape[0]
-    cache_dev = kv.shape[1]
+    rows_all = q_ref.shape[0] * heads
+    cache_dev = kv.shape[2]
     half = LATENT // 2
     chunks = rows_all // chunk
     per_request = qtok * heads // chunk
@@ -130,11 +130,10 @@
         b = c // per_request
         first_token = lax.rem(c, per_request) * tokens
         limits = [lengths[b] - (qtok - 1) + offsets[b, first_token + t] - start for t in range(tokens)]
-        q = q_ref[pl.ds(pl.multiple_of(c * chunk, chunk), chunk), :]
+        q = jnp.concatenate([q_ref[c * tokens + t].T for t in range(tokens)], axis=0)
         peak = jnp.full((chunk, LANES), -1e30, jnp.float32)
         for j in range(cache_dev // span):
-            s = lax.dot_general(q, kv[b, j * span:(j + 1) * span, :], (((1,), (1,)), ((), ())),
-                                preferred_element_type=jnp.float32)
+            s = jnp.dot(q, kv[b, :, j * span:(j + 1) * span], preferred_element_type=jnp.float32)
             places = lax.broadcasted_iota(jnp.int32, (heads, span), 1) + j * span
             s = jnp.concatenate(
                 [jnp.where(places < limits[t], s[t * heads:(t + 1) * heads] * SCALE2, -1e30)
@@ -150,9 +149,9 @@
             w = jnp.exp2(score[:, j * value_span:(j + 1) * value_span] - base)
             for i in range(value_span // LANES):
                 total = total + w[:, i * LANES:(i + 1) * LANES]
-            value = value + jnp.dot(w.astype(jnp.bfloat16),
-                                    kv[b, j * value_span:(j + 1) * value_span, :LATENT],
-                                    preferred_element_type=jnp.float32)
+            value = value + lax.dot_general(
+                w.astype(jnp.bfloat16), kv[b, :LATENT, j * value_span:(j + 1) * value_span],
+                (((1,), (1,)), ((), ())), preferred_element_type=jnp.float32)
         total = jnp.sum(total, axis=1, keepdims=True)
         for h in range(2):
             with_meta((c, h), w0, value[:, h * half:(h + 1) * half], peak, total, half)
@@ -260,7 +259,7 @@
         ],
         out_specs=pl.BlockSpec(memory_space=pltpu.VMEM),
         scratch_shapes=[
-            pltpu.VMEM((requests, cache_dev, width), jnp.bfloat16),
+            pltpu.VMEM((requests, width, cache_dev), jnp.bfloat16),
             pltpu.VMEM((chunk, cache_dev), jnp.float32),
             pltpu.VMEM((chunks, 2, chunk, wide), jnp.float32),
             pltpu.VMEM((chunks, chunk, wide), jnp.float32),
@@ -274,7 +273,8 @@
         compiler_params=pltpu.CompilerParams(
             collective_id=0, has_side_effects=True, vmem_limit_bytes=60 * 1024 * 1024),
         name="latent_attention",
-    )(lengths, offsets, queries.reshape(rows, width), latent_cache)
+    )(lengths, offsets, jnp.swapaxes(queries, 2, 3).reshape(requests * qtok, width, heads),
+      jnp.swapaxes(latent_cache, 1, 2))
     return out.reshape(requests, qtok, heads, LATENT)
 
 

time: 73.3 us -> 56.6 us (0.77)
  local copies, waits for them, and re-layouts: 18.3 us -> 2.26 us
    unnamed x3 -> x1, local copies, waits for them, and re-layouts: 18.3 us -> 2.26 us
where the time goes in v2:
time: 56.6 us; the launch traced here: 56.5 us
  Pallas kernels  54.2 us (96%)
  local copies, waits for them, and re-layouts  2.26 us (4%)
    pallas_call x1, Pallas kernels, on_device(): pl.pallas_call(functools.partial(kernel, n, qtok, heads, chunk), out_shap...  54.2 us
    unnamed x1, local copies, waits for them, and re-layouts  2.26 us

profile of v2, /device:TPU:0, one launch (start us, length us, event | category | flops | bytes accessed | tf_op | source)
XLA Modules:
  0.0 56.5 jit_solution(2516178574135609087)
XLA Ops:
  0.0 54.2 %latent_attention.1 = bf16[1024,512]{1,0:T(8,128)(2,1)} custom-call(s32[2]{0:T(128)} %lengths.1, s32[2,4]{1,0:T(2,128)} %offsets.1, bf16[8,576,128]{2,1,0:T(8,128)(2,1)} %bitcast.7, bf16[2,576,4096]{2,1,0:T(8,128)(2,1)} %bitcast.5), custom_call_target="tpu_custom_call" | custom-call | tf_op jit(solution)/shard_map/latent_attention/pallas_call | solution.py:251
  54.2 2.3 %copy.6 = bf16[2,4,128,512]{3,2,1,0:T(8,128)(2,1)} copy(bf16[2,4,128,512]{3,2,1,0:T(8,128)(2,1)} %bitcast.6) | data formatting | bytes 2097152

commit v3 on v2

--- a/solution.py
+++ b/solution.py
@@ -44,7 +44,8 @@
 
 
 def kernel(n, qtok, heads, chunk, lengths, offsets, q_ref, cache_hbm, out_ref,
-           kv, score, w0, core_in, works, stage_in, gathered, load_sem, send_sem, recv_sem):
+           kv, score, w0, core_in, works, stage_in, meta, meta_in, factors, gathered,
+           load_sem, send_sem, recv_sem):
     rows_all = q_ref.shape[0] * heads
     cache_dev = kv.shape[2]
     half = LATENT // 2
@@ -105,6 +106,19 @@
         src = works[stage].at[j, pl.ds(other * rows, rows)]
         return remote(src, stage_in[stage].at[j, d - 1], j, 1 + 3 * stage + d - 1, device)
 
+    def meta_copy(j, stage, d):
+        _, device = peer(stage, d)
+        slot = 2 + 6 * stages + 3 * stage + d - 1
+        return remote(meta[stage].at[j], meta_in[stage].at[j, d - 1], j, slot, device)
+
+    def send_stage(j, stage):
+        for d in range(1, radices[stage]):
+            meta_copy(j, stage, d).start()
+            stage_copy(j, stage, d).start()
+
+    def pack(top, total):
+        return jnp.where(lax.broadcasted_iota(jnp.int32, (8, chunk), 0) == 0, top, total)
+
     def first_piece(stage):
         return sum(digits[i] * blocks[i] for i in range(stage + 1))
 
@@ -142,6 +156,11 @@
             for i in range(span // LANES):
                 peak = jnp.maximum(peak, s[:, i * LANES:(i + 1) * LANES])
         peak = jnp.max(peak, axis=1, keepdims=True)
+
+        @pl.when(c >= 1)
+        def _():
+            receive_core(c - 1)
+
         base = jnp.maximum(peak, -1e29)
         total = jnp.zeros((chunk, LANES), jnp.float32)
         value = jnp.zeros((chunk, LATENT), jnp.float32)
@@ -160,24 +179,39 @@
     def receive_core(j):
         core_copy(j).wait_recv()
         value, top, total = combine([w0[j, core], core_in[j]], half)
-        with_meta((j,), works[0], value, top, total, half)
-        for d in range(1, radices[0]):
-            stage_copy(j, 0, d).start()
+        works[0][j] = value
+        lane = lax.broadcasted_iota(jnp.int32, (chunk, LANES), 1)
+        turned = jnp.where(lane < 64, top, total).T
+        meta[0][j] = pack(turned[:8], turned[64:72])
+        send_stage(j, 0)
 
     def receive_stage(j, stage):
-        for d in range(1, radices[stage]):
+        radix = radices[stage]
+        for d in range(1, radix):
+            meta_copy(j, stage, d).wait_recv()
+        metas = [meta[stage][j]] + [meta_in[stage][j, d - 1] for d in range(1, radix)]
+        top = functools.reduce(jnp.maximum, [m[0:1] for m in metas])
+        shares = [jnp.exp2(m[0:1] - top) for m in metas]
+        total = sum(m[1:2] * f for m, f in zip(metas, shares))
+        if stage + 1 == stages:
+            shares = [f / total for f in shares]
+        segment = LANES // radix
+        factors[...] = jnp.concatenate(
+            [jnp.broadcast_to(f, (segment, chunk)) for f in shares], axis=0).T
+        rows = stage_in[stage].shape[2]
+        first = pl.multiple_of(first_piece(stage) * piece_rows, piece_rows)
+        mine = factors[pl.ds(first, rows), :]
+        value = works[stage][j, pl.ds(pl.multiple_of(digits[stage] * rows, rows), rows), :] * mine[:, 0:1]
+        for d in range(1, radix):
             stage_copy(j, stage, d).wait_recv()
-        rows = stage_in[stage].shape[2]
-        mine = works[stage][j, pl.ds(pl.multiple_of(digits[stage] * rows, rows), rows), :]
-        value, top, total = combine(
-            [mine] + [stage_in[stage][j, d - 1] for d in range(1, radices[stage])], half)
+            value = value + stage_in[stage][j, d - 1] * mine[:, d * segment:d * segment + 1]
         if stage + 1 < stages:
-            with_meta((j,), works[stage + 1], value, top, total, half)
-            for d in range(1, radices[stage + 1]):
-                stage_copy(j, stage + 1, d).start()
+            works[stage + 1][j] = value
+            meta[stage + 1][j] = pack(top, total)
+            send_stage(j, stage + 1)
         else:
-            gathered[j, core, first_piece(stage)] = (value / total).astype(jnp.bfloat16)
-            for d in range(1, radices[stage]):
+            gathered[j, core, first_piece(stage)] = value.astype(jnp.bfloat16)
+            for d in range(1, radix):
                 gather_copy(j, stage, d).start()
 
     def receive_gather(j, stage):
@@ -198,11 +232,11 @@
         for stage in range(stages):
             for d in range(1, radices[stage]):
                 stage_copy(j, stage, d).wait_send()
+                meta_copy(j, stage, d).wait_send()
                 gather_copy(j, stage, d).wait_send()
         core_gather(j, core).wait_send()
 
-    steps = [receive_core]
-    steps += [functools.partial(receive_stage, stage=s) for s in range(stages)]
+    steps = [functools.partial(receive_stage, stage=s) for s in range(stages)]
     steps += [functools.partial(receive_gather, stage=s) for s in reversed(range(stages))]
     steps += [finish]
 
@@ -220,16 +254,20 @@
 
             compute(i)
 
-        for lag in range(len(steps), 0, -1):
+        @pl.when(i == chunks)
+        def _():
+            receive_core(chunks - 1)
+
+        for lag, step in enumerate(steps, 3):
             j = i - lag
 
             @pl.when(jnp.logical_and(j >= 0, j < chunks))
             def _():
-                steps[lag - 1](j)
+                step(j)
 
         return carry
 
-    lax.fori_loop(0, chunks + len(steps), iteration, 0)
+    lax.fori_loop(0, chunks + len(steps) + 2, iteration, 0)
 
 
 def on_device(n, queries, latent_cache, lengths, offsets):
@@ -242,12 +280,14 @@
     chunks = rows // chunk
     half = LATENT // 2
     wide = half + LANES
-    works, stage_in, left = [], [], chunk
+    works, stage_in, meta, meta_in, left = [], [], [], [], chunk
     for radix in radices:
-        works.append(pltpu.VMEM((chunks, left, wide), jnp.float32))
+        works.append(pltpu.VMEM((chunks, left, half), jnp.float32))
         left //= radix
-        stage_in.append(pltpu.VMEM((chunks, radix - 1, left, wide), jnp.float32))
-    slots = 2 + 6 * stages
+        stage_in.append(pltpu.VMEM((chunks, radix - 1, left, half), jnp.float32))
+        meta.append(pltpu.VMEM((chunks, 8, chunk), jnp.float32))
+        meta_in.append(pltpu.VMEM((chunks, radix - 1, 8, chunk), jnp.float32))
+    slots = 2 + 9 * stages
     out = pl.pallas_call(
         functools.partial(kernel, n, qtok, heads, chunk),
         out_shape=jax.ShapeDtypeStruct((rows, LATENT), jnp.bfloat16),
@@ -265,6 +305,9 @@
             pltpu.VMEM((chunks, chunk, wide), jnp.float32),
             works,
             stage_in,
+            meta,
+            meta_in,
+            pltpu.VMEM((chunk, LANES), jnp.float32),
             pltpu.VMEM((chunks, 2, n // 2, chunk // (n // 2), half), jnp.bfloat16),
             pltpu.SemaphoreType.DMA((requests,)),
             pltpu.SemaphoreType.DMA((chunks, slots)),

time: 56.6 us -> 48 us (0.85)
  Pallas kernels: 54.2 us -> 45.6 us
    pallas_call x1, Pallas kernels: 54.2 us -> 45.6 us  [on_device(): pl.pallas_call(functools.partial(kernel, n, qtok, heads, chunk), out_shap...]
where the time goes in v3:
time: 48 us; the launch traced here: 47.9 us
  Pallas kernels  45.6 us (95%)
  local copies, waits for them, and re-layouts  2.26 us (5%)
    pallas_call x1, Pallas kernels, on_device(): pl.pallas_call(functools.partial(kernel, n, qtok, heads, chunk), out_shap...  45.6 us
    unnamed x1, local copies, waits for them, and re-layouts  2.26 us

profile of v3, /device:TPU:0, one launch (start us, length us, event | category | flops | bytes accessed | tf_op | source)
XLA Modules:
  0.0 47.9 jit_solution(15956146705750640848)
XLA Ops:
  0.0 45.6 %latent_attention.1 = bf16[1024,512]{1,0:T(8,128)(2,1)} custom-call(s32[2]{0:T(128)} %lengths.1, s32[2,4]{1,0:T(2,128)} %offsets.1, bf16[8,576,128]{2,1,0:T(8,128)(2,1)} %bitcast.7, bf16[2,576,4096]{2,1,0:T(8,128)(2,1)} %bitcast.5), custom_call_target="tpu_custom_call" | custom-call | tf_op jit(solution)/shard_map/latent_attention/pallas_call | solution.py:291
  45.6 2.3 %copy.6 = bf16[2,4,128,512]{3,2,1,0:T(8,128)(2,1)} copy(bf16[2,4,128,512]{3,2,1,0:T(8,128)(2,1)} %bitcast.6) | data formatting | bytes 2097152

commit v4 on v3

--- a/solution.py
+++ b/solution.py
@@ -69,21 +69,38 @@
     digits = [lax.rem(chip // s, r) for s, r in zip(strides, radices)]
     partner = me + 1 - 2 * core
 
-    def peer(stage, d):
-        other = lax.rem(digits[stage] + d, radices[stage])
-        return other, me + (other - digits[stage]) * strides[stage] * 2
+    even = len(set(radices)) == 1
+
+    def turned_order(j, values, stage):
+        if not even:
+            return values[stage]
+        swap = lax.rem(j, 2) * (1 - j // 2)
+        return values[stage] + swap * (values[stages - 1 - stage] - values[stage])
+
+    def digit(j, stage):
+        return turned_order(j, digits, stage)
+
+    def peer(j, stage, d):
+        mine = digit(j, stage)
+        other = lax.rem(mine + d, radices[stage])
+        return other, me + (other - mine) * turned_order(j, strides, stage) * 2
 
     barrier = pltpu.get_barrier_semaphore()
     peers = [partner]
     for stage in range(stages):
-        peers += [peer(stage, d)[1] for d in range(1, radices[stage])]
+        peers += [peer(0, stage, d)[1] for d in range(1, radices[stage])]
     for device in peers:
         pl.semaphore_signal(barrier, inc=1, device_id=(device,), device_id_type=MESH)
 
-    def load(b):
-        return pltpu.make_async_copy(cache_hbm.at[b], kv.at[b], load_sem.at[b])
-
-    load(0).start()
+    load_parts = 4
+    load_span = cache_dev // load_parts
+
+    def load(b, part):
+        where = (b, slice(None), pl.ds(part * load_span, load_span))
+        return pltpu.make_async_copy(cache_hbm.at[where], kv.at[where], load_sem.at[b, part])
+
+    for part in range(load_parts):
+        load(0, part).start()
     pl.semaphore_wait(barrier, len(peers))
 
     start = me * cache_dev
@@ -99,7 +116,7 @@
         return remote(w0.at[j, 1 - core], core_in.at[j], j, 0, partner)
 
     def stage_copy(j, stage, d):
-        other, device = peer(stage, d)
+        other, device = peer(j, stage, d)
         rows = chunk
         for r in radices[:stage + 1]:
             rows //= r
@@ -107,7 +124,7 @@
         return remote(src, stage_in[stage].at[j, d - 1], j, 1 + 3 * stage + d - 1, device)
 
     def meta_copy(j, stage, d):
-        _, device = peer(stage, d)
+        _, device = peer(j, stage, d)
         slot = 2 + 6 * stages + 3 * stage + d - 1
         return remote(meta[stage].at[j], meta_in[stage].at[j, d - 1], j, slot, device)
 
@@ -119,20 +136,20 @@
     def pack(top, total):
         return jnp.where(lax.broadcasted_iota(jnp.int32, (8, chunk), 0) == 0, top, total)
 
-    def first_piece(stage):
-        return sum(digits[i] * blocks[i] for i in range(stage + 1))
+    def first_piece(j, stage):
+        return sum(digit(j, i) * blocks[i] for i in range(stage + 1))
 
     def gather_copy(j, stage, d):
-        _, device = peer(stage, d)
-        ref = gathered.at[j, core, pl.ds(first_piece(stage), blocks[stage])]
+        _, device = peer(j, stage, d)
+        ref = gathered.at[j, core, pl.ds(first_piece(j, stage), blocks[stage])]
         return remote(ref, ref, j, 1 + 3 * stages + 3 * stage + d - 1, device)
 
     def gather_arrival(j, stage, d):
-        _, device = peer(stage, d)
-        origin = lax.rem(digits[stage] + radices[stage] - d, radices[stage])
+        _, device = peer(j, stage, d)
+        origin = lax.rem(digit(j, stage) + radices[stage] - d, radices[stage])
         first = origin * blocks[stage]
         if stage:
-            first = first + first_piece(stage - 1)
+            first = first + first_piece(j, stage - 1)
         ref = gathered.at[j, core, pl.ds(first, blocks[stage])]
         return remote(ref, ref, j, 1 + 3 * stages + 3 * stage + d - 1, device)
 
@@ -146,7 +163,13 @@
         limits = [lengths[b] - (qtok - 1) + offsets[b, first_token + t] - start for t in range(tokens)]
         q = jnp.concatenate([q_ref[c * tokens + t].T for t in range(tokens)], axis=0)
         peak = jnp.full((chunk, LANES), -1e30, jnp.float32)
+        fresh = lax.rem(c, per_request) == 0
         for j in range(cache_dev // span):
+            if j * span % load_span == 0:
+                @pl.when(fresh)
+                def _():
+                    load(b, j * span // load_span).wait()
+
             s = jnp.dot(q, kv[b, :, j * span:(j + 1) * span], preferred_element_type=jnp.float32)
             places = lax.broadcasted_iota(jnp.int32, (heads, span), 1) + j * span
             s = jnp.concatenate(
@@ -156,6 +179,11 @@
             for i in range(span // LANES):
                 peak = jnp.maximum(peak, s[:, i * LANES:(i + 1) * LANES])
         peak = jnp.max(peak, axis=1, keepdims=True)
+
+        @pl.when(jnp.logical_and(fresh, b + 1 < kv.shape[0]))
+        def _():
+            for part in range(load_parts):
+                load(b + 1, part).start()
 
         @pl.when(c >= 1)
         def _():
@@ -199,9 +227,9 @@
         factors[...] = jnp.concatenate(
             [jnp.broadcast_to(f, (segment, chunk)) for f in shares], axis=0).T
         rows = stage_in[stage].shape[2]
-        first = pl.multiple_of(first_piece(stage) * piece_rows, piece_rows)
+        first = pl.multiple_of(first_piece(j, stage) * piece_rows, piece_rows)
         mine = factors[pl.ds(first, rows), :]
-        value = works[stage][j, pl.ds(pl.multiple_of(digits[stage] * rows, rows), rows), :] * mine[:, 0:1]
+        value = works[stage][j, pl.ds(pl.multiple_of(digit(j, stage) * rows, rows), rows), :] * mine[:, 0:1]
         for d in range(1, radix):
             stage_copy(j, stage, d).wait_recv()
             value = value + stage_in[stage][j, d - 1] * mine[:, d * segment:d * segment + 1]
@@ -210,7 +238,7 @@
             meta[stage + 1][j] = pack(top, total)
             send_stage(j, stage + 1)
         else:
-            gathered[j, core, first_piece(stage)] = value.astype(jnp.bfloat16)
+            gathered[j, core, first_piece(j, stage)] = value.astype(jnp.bfloat16)
             for d in range(1, radix):
                 gather_copy(j, stage, d).start()
 
@@ -243,15 +271,6 @@
     def iteration(i, carry):
         @pl.when(i < chunks)
         def _():
-            @pl.when(lax.rem(i, per_request) == 0)
-            def _():
-                b = i // per_request
-                load(b).wait()
-
-                @pl.when(b + 1 < kv.shape[0])
-                def _():
-                    load(b + 1).start()
-
             compute(i)
 
         @pl.when(i == chunks)
@@ -309,7 +328,7 @@
             meta_in,
             pltpu.VMEM((chunk, LANES), jnp.float32),
             pltpu.VMEM((chunks, 2, n // 2, chunk // (n // 2), half), jnp.bfloat16),
-            pltpu.SemaphoreType.DMA((requests,)),
+            pltpu.SemaphoreType.DMA((requests, 4)),
             pltpu.SemaphoreType.DMA((chunks, slots)),
             pltpu.SemaphoreType.DMA((chunks, slots)),
         ],

time: 48 us -> 50.7 us (1.056)
  Pallas kernels: 45.6 us -> 48.2 us
    pallas_call x1, Pallas kernels: 45.6 us -> 48.2 us  [on_device(): pl.pallas_call(functools.partial(kernel, n, qtok, heads, chunk), out_shap...]
where the time goes in v4:
time: 50.7 us; the launch traced here: 50.5 us
  Pallas kernels  48.2 us (95%)
  local copies, waits for them, and re-layouts  2.26 us (4%)
    pallas_call x1, Pallas kernels, on_device(): pl.pallas_call(functools.partial(kernel, n, qtok, heads, chunk), out_shap...  48.2 us
    unnamed x1, local copies, waits for them, and re-layouts  2.26 us

profile of v4, /device:TPU:0, one launch (start us, length us, event | category | flops | bytes accessed | tf_op | source)
XLA Modules:
  0.0 50.5 jit_solution(5834793978517558707)
XLA Ops:
  0.0 48.2 %latent_attention.1 = bf16[1024,512]{1,0:T(8,128)(2,1)} custom-call(s32[2]{0:T(128)} %lengths.1, s32[2,4]{1,0:T(2,128)} %offsets.1, bf16[8,576,128]{2,1,0:T(8,128)(2,1)} %bitcast.7, bf16[2,576,4096]{2,1,0:T(8,128)(2,1)} %bitcast.5), custom_call_target="tpu_custom_call" | custom-call | tf_op jit(solution)/shard_map/latent_attention/pallas_call | solution.py:310
  48.2 2.3 %copy.6 = bf16[2,4,128,512]{3,2,1,0:T(8,128)(2,1)} copy(bf16[2,4,128,512]{3,2,1,0:T(8,128)(2,1)} %bitcast.6) | data formatting | bytes 2097152
